TPU v7x, 32 devices: a whole 2x2x4 slice. The times are simulated.
32 devices in a mesh: gx: 4 (over y, x), gy: 2 (over core), gz: 4 (over z).
Axes of the slice: x: 2, y: 2, z: 4, core: 2. Of those that a mesh axis runs over, the one named last changes fastest.
Arguments:
- pair: bfloat16 [128, 1024, 1024], P('gz', 'gy', 'gx'), may hold values from -6 to 6
- pair_mask: int32 [1024, 1024], P('gy', 'gx'), may hold values 0 or 1
- in_gain: float32 [128], replicated, may hold values from 0.5 to 2
- w_left: bfloat16 [128, 128], P(None, 'gz'), may hold values from -0.5 to 0.5
- w_left_gate: bfloat16 [128, 128], P(None, 'gz'), may hold values from -0.5 to 0.5
- w_right: bfloat16 [128, 128], P(None, 'gz'), may hold values from -0.5 to 0.5
- w_right_gate: bfloat16 [128, 128], P(None, 'gz'), may hold values from -0.5 to 0.5
- w_out_gate: bfloat16 [128, 128], P(None, 'gz'), may hold values from -0.5 to 0.5
- out_gain: float32 [128], P('gz'), may hold values from 0.5 to 2
- w_out: bfloat16 [128, 128], P(None, 'gz'), may hold values from -0.5 to 0.5
Outputs:
- update: bfloat16 [128, 1024, 1024], P('gz', 'gy', 'gx')
All inputs are finite; a program needn't handle non-finite values. No bound on the sum of `pair_mask` on one device may be relied on, other than what follows from the above.
Results may differ from a plain program's by a relative error of at most 0.0078.
Values may be sent and summed in bfloat16 or wider, within the bound.
No kernel may reach another device: no remote copies, remote signals or barrier semaphores. Data moves between devices by JAX's collectives and lax.ppermute only.
A program may use at most 192 MiB of HBM per device.

v0:
```python
import jax
import jax.numpy as jnp
from jax import lax
from jax.sharding import PartitionSpec as P

epsilon = 1e-05


def local(
    pair,
    pair_mask,
    in_gain,
    w_left,
    w_left_gate,
    w_right,
    w_right_gate,
    w_out_gate,
    out_gain,
    w_out,
):
    gathered = lax.all_gather(pair, "gz", axis=0, tiled=True).astype(jnp.float32)
    average = jnp.mean(gathered, axis=0)
    centered = gathered - average
    spread = jnp.mean(jnp.square(centered), axis=0)
    normed = (centered * lax.rsqrt(spread + epsilon) * in_gain[:, None, None]).astype(jnp.bfloat16)
    mask_float = pair_mask.astype(jnp.float32)[None]

    def project(weight):
        return jnp.einsum("cik,ch->hik", normed, weight, preferred_element_type=jnp.float32)

    left_rows = (mask_float * jax.nn.sigmoid(project(w_left_gate)) * project(w_left)).astype(
        jnp.bfloat16
    )
    right_rows = (mask_float * jax.nn.sigmoid(project(w_right_gate)) * project(w_right)).astype(
        jnp.bfloat16
    )
    out_gate = jax.nn.sigmoid(
        jnp.einsum("cij,cd->dij", normed, w_out_gate, preferred_element_type=jnp.float32)
    )
    left_group, right_group = (
        lax.all_to_all(left_rows, "gx", split_axis=0, concat_axis=2, tiled=True),
        lax.all_to_all(right_rows, "gx", split_axis=0, concat_axis=2, tiled=True),
    )
    full_product = lax.dot_general(
        left_group,
        lax.all_gather(right_group, "gy", axis=1, tiled=True),
        (((2,), (2,)), ((0,), (0,))),
        preferred_element_type=jnp.float32,
    )
    mixed_sum = lax.all_to_all(full_product, "gx", split_axis=2, concat_axis=0, tiled=True)
    channel_count = lax.axis_size("gz") * mixed_sum.shape[0]
    sum_terms = lax.psum(jnp.sum(mixed_sum, axis=0), "gz")
    mix_average = sum_terms / channel_count
    mix_centered = mixed_sum - mix_average
    mix_spread = lax.psum(jnp.sum(jnp.square(mix_centered), axis=0), "gz") / channel_count
    local_mix = (mix_centered * lax.rsqrt(mix_spread + epsilon) * out_gain[:, None, None]).astype(
        jnp.bfloat16
    )
    normed_mix = lax.all_gather(local_mix, "gz", axis=0, tiled=True)
    projected = jnp.einsum("hij,hd->dij", normed_mix, w_out, preferred_element_type=jnp.float32)
    return (out_gate * projected).astype(jnp.bfloat16)


def solution(mesh):
    placed = (
        P("gz", "gy", "gx"),
        P("gy", "gx"),
        P(),
        P(None, "gz"),
        P(None, "gz"),
        P(None, "gz"),
        P(None, "gz"),
        P(None, "gz"),
        P("gz"),
        P(None, "gz"),
    )
    return jax.shard_map(
        local, mesh=mesh, in_specs=placed, out_specs=P("gz", "gy", "gx"), check_vma=False
    )
```

profile of v0, /device:TPU:0, one launch (start us, length us, event | category | flops | bytes accessed | tf_op | source)
XLA Modules:
  0.0 1984.1 jit_solution(8913950968688597543)
XLA Ops:
  7.3 1.1 convert_element_type.23
  8.4 564.6 %all-gather.4.cloned.1.call-done = bf16[128,512,256]{2,1,0:T(8,128)(2,1)} async-done(((bf16[32,512,256]{2,1,0:T(8,128)(2,1)}), bf16[128,512,256]{2,1,0:T(8,128)(2,1)}) %all-gather.4.cloned.1.call-update) | async-done | bytes 33554448 | tf_op jit(solution)/shard_map/all_gather | solution.py:21
  573.0 11.4 convert_reduce_fusion
  584.5 11.7 fusion.2
  596.2 23.0 %fusion.4 = bf16[128,512,256]{2,1,0:T(8,128)(2,1)} fusion(bf16[128,512,256]{2,1,0:T(8,128)(2,1)} %all-gather.4.cloned.1.call-done, f32[128]{0:T(128)S(1)} %copy-done.4, f32[512,256]{1,0:T(8,128)S(1)} %add_rsqrt_fusion.1, f32[512,256]{1,0:T(8,128)S(1)} %broadcast_multiply_fusion.1), kind=kLoop, calls=%fused_computation.6 | loop fusion | flops 83886080 | bytes 68157952 | tf_op jit(solution)/shard_map/convert_element_type | solution.py:25
  619.3 35.7 %fusion.11 = f32[512,256,32]{1,2,0:T(8,128)} fusion(bf16[128,512,256]{2,1,0:T(8,128)(2,1)} %fusion.4, bf16[128,32]{0,1:T(8,128)(2,1)S(1)} %copy-done), kind=kOutput, calls=%fused_computation.13 | convolution fusion | flops 1073741824 | bytes 50339840 | tf_op jit(solution)/shard_map/cik,ch->hik/dot_general | solution.py:29
  655.0 38.1 %fusion.28 = bf16[32,512,256]{2,0,1:T(8,128)(2,1)} fusion(bf16[128,512,256]{2,1,0:T(8,128)(2,1)} %fusion.4, f32[512,256,32]{1,2,0:T(8,128)} %fusion.11, f32[512,256]{1,0:T(8,128)S(1)} %convert_element_type.23, bf16[128,32]{0,1:T(8,128)(2,1)S(1)} %copy-done.6), kind=kOutput, calls=%fused_computation.32 | convolution fusion | flops 1098907648 | bytes 59252736 | tf_op jit(solution)/shard_map/cik,ch->hik/dot_general | solution.py:29
  693.1 11.4 copy.27
  704.5 97.4 %all_to_all.54 = bf16[32,512,256]{2,1,0:T(8,128)(2,1)S(1)} all-to-all(bf16[32,512,256]{2,1,0:T(8,128)(2,1)} %copy.27), channel_id=1, replica_groups=mesh['gx'=4,'gy'=2,'gz'=4] {'gx'}, dimensions={0} | all-to-all | bytes 16777216 | tf_op jit(solution)/shard_map/all_to_all | solution.py:42
  801.8 7.3 copy.52
  809.1 14.3 all_to_all.46
  823.5 37.6 %fusion.7 = f32[512,256,32]{1,2,0:T(8,128)} fusion(bf16[128,512,256]{2,1,0:T(8,128)(2,1)} %fusion.4, bf16[128,32]{0,1:T(8,128)(2,1)S(1)} %copy-done.2), kind=kOutput, calls=%fused_computation.9 | convolution fusion | flops 1073741824 | bytes 50339840 | tf_op jit(solution)/shard_map/cik,ch->hik/dot_general | solution.py:29
  861.2 38.1 %fusion.25 = bf16[32,512,256]{2,0,1:T(8,128)(2,1)} fusion(bf16[128,512,256]{2,1,0:T(8,128)(2,1)} %fusion.4, f32[512,256,32]{1,2,0:T(8,128)} %fusion.7, f32[512,256]{1,0:T(8,128)S(1)} %convert_element_type.23, bf16[128,32]{0,1:T(8,128)(2,1)S(1)} %copy-done.7), kind=kOutput, calls=%fused_computation.31 | convolution fusion | flops 1098907648 | bytes 59252736 | tf_op jit(solution)/shard_map/cik,ch->hik/dot_general | solution.py:29
  899.3 11.4 copy.23
  910.7 94.8 %all_to_all.55 = bf16[32,512,256]{2,1,0:T(8,128)(2,1)S(1)} all-to-all(bf16[32,512,256]{2,1,0:T(8,128)(2,1)} %copy.23), channel_id=1, replica_groups=mesh['gx'=4,'gy'=2,'gz'=4] {'gx'}, dimensions={0} | all-to-all | bytes 16777216 | tf_op jit(solution)/shard_map/all_to_all | solution.py:41
  1005.5 7.3 copy.53
  1012.8 14.3 all_to_all.42
  1027.1 17.0 fusion.37
  1044.0 17.6 copy.29
  1061.6 190.6 %all_to_all.56 = f32[8,512,1024]{1,0,2:T(8,128)} all-to-all(f32[8,512,1024]{1,0,2:T(8,128)} %copy.29), channel_id=1, replica_groups=mesh['gx'=4,'gy'=2,'gz'=4] {'gx'}, dimensions={2} | all-to-all | bytes 33554432 | tf_op jit(solution)/shard_map/all_to_all | solution.py:50
  1252.3 20.2 %copy.30 = f32[8,512,4,256]{3,0,2,1:T(8,128)} copy(f32[8,512,4,256]{1,0,3,2:T(8,128)} %bitcast.52) | data formatting | bytes 33554432 | tf_op jit(solution)/shard_map/all_to_all | solution.py:50
  1272.5 9.5 bitcast_reduce_fusion
  1282.1 36.2 %all-reduce.3.cloned.1.call-done = f32[512,256]{1,0:T(8,128)} async-done(((f32[512,256]{1,0:T(8,128)}), f32[512,256]{1,0:T(8,128)}) %all-reduce.3.cloned.1.call-update) | async-done | bytes 524304 | tf_op jit(solution)/shard_map/psum | solution.py:52
  1318.2 1.1 broadcast_multiply_fusion
  1319.3 12.2 fusion.19
  1331.6 38.6 %all-reduce.5.cloned.1.call-done = f32[512,256]{1,0:T(8,128)} async-done(((f32[512,256]{1,0:T(8,128)}), f32[512,256]{1,0:T(8,128)}) %all-reduce.5.cloned.1.call-update) | async-done | bytes 524304 | tf_op jit(solution)/shard_map/psum | solution.py:55
  1370.1 1.1 add_rsqrt_fusion
  1371.3 11.1 fusion.17
  1382.4 35.8 %fusion.5 = f32[512,256,32]{1,2,0:T(8,128)} fusion(bf16[128,512,256]{2,1,0:T(8,128)(2,1)} %fusion.4, bf16[128,32]{0,1:T(8,128)(2,1)S(1)} %copy-done.3), kind=kOutput, calls=%fused_computation.7 | convolution fusion | flops 1073741824 | bytes 50339840 | tf_op jit(solution)/shard_map/cij,cd->dij/dot_general | solution.py:38
  1418.2 525.5 %all-gather.8.cloned.1.call-done = bf16[128,512,256]{2,0,1:T(8,128)(2,1)} async-done(((bf16[32,512,256]{2,0,1:T(8,128)(2,1)}), bf16[128,512,256]{2,0,1:T(8,128)(2,1)}) %all-gather.8.cloned.1.call-update) | async-done | bytes 33554448 | tf_op jit(solution)/shard_map/all_gather | solution.py:59
  1943.8 21.8 %fusion.24 = bf16[32,512,256]{2,0,1:T(8,128)(2,1)} fusion(bf16[128,512,256]{2,0,1:T(8,128)(2,1)} %all-gather.8.cloned.1.call-done, f32[512,256,32]{1,2,0:T(8,128)} %fusion.5, bf16[128,32]{0,1:T(8,128)(2,1)S(1)} %copy-done.8), kind=kOutput, calls=%fused_computation.30 | convolution fusion | flops 1094713344 | bytes 58728448 | tf_op jit(solution)/shard_map/hij,hd->dij/dot_general | solution.py:60
  1965.6 11.5 copy.31
  (31 shorter events, 1.1 us)
Async XLA Ops:
  6.5 612.8 %copy-start = (bf16[128,32]{0,1:T(8,128)(2,1)S(1)}, bf16[128,32]{0,1:T(8,128)(2,1)}, u32[]{:S(2)}) copy-start(bf16[128,32]{0,1:T(8,128)(2,1)} %param.16) | copy-start | bytes 24580
  6.5 566.5 %all-gather.4.cloned.1.call-start = ((), (), s32[]{:S(2)}) async-start(), calls=%async_computation.3 | async-start | bytes 41943040 | tf_op jit(solution)/shard_map/all_gather | solution.py:21
  7.3 1019.8 %all-gather.6.cloned.1.call-start = ((), (), s32[]{:S(2)}) async-start(), calls=%async_computation.4 | async-start | bytes 25165824 | tf_op jit(solution)/shard_map/all_gather | solution.py:46
  584.5 11.8 copy-start.4
  619.3 35.7 %copy-start.6 = (bf16[128,32]{0,1:T(8,128)(2,1)S(1)}, bf16[128,32]{0,1:T(8,128)(2,1)}, u32[]{:S(2)}) copy-start(bf16[128,32]{0,1:T(8,128)(2,1)} %param.15) | copy-start | bytes 24580
  809.1 14.4 copy-start.2
  823.5 37.7 %copy-start.7 = (bf16[128,32]{0,1:T(8,128)(2,1)S(1)}, bf16[128,32]{0,1:T(8,128)(2,1)}, u32[]{:S(2)}) copy-start(bf16[128,32]{0,1:T(8,128)(2,1)} %param.13) | copy-start | bytes 24580
  823.5 494.7 %all-reduce.3.cloned.1.call-start = ((), (), s32[]{:S(2)}) async-start(), calls=%async_computation.5 | async-start | bytes 1048576 | tf_op jit(solution)/shard_map/psum | solution.py:52
  1272.5 98.7 %copy-start.5 = (f32[32]{0:T(128)S(1)}, f32[32]{0:T(128)}, u32[]{:S(2)}) copy-start(f32[32]{0:T(128)} %param.18) | copy-start | bytes 388
  1282.0 88.1 %all-reduce.5.cloned.1.call-start = ((), (), s32[]{:S(2)}) async-start(), calls=%async_computation.6 | async-start | bytes 1048576 | tf_op jit(solution)/shard_map/psum | solution.py:55
  1331.5 612.2 %all-gather.8.cloned.1.call-start = ((), (), s32[]{:S(2)}) async-start(), calls=%async_computation.7 | async-start | bytes 41943040 | tf_op jit(solution)/shard_map/all_gather | solution.py:59
  1371.3 11.1 copy-start.3
  1382.4 561.3 %copy-start.8 = (bf16[128,32]{0,1:T(8,128)(2,1)S(1)}, bf16[128,32]{0,1:T(8,128)(2,1)}, u32[]{:S(2)}) copy-start(bf16[128,32]{0,1:T(8,128)(2,1)} %param.19) | copy-start | bytes 24580
  1943.7 33.4 %copy-start.1 = (bf16[128,32]{0,1:T(8,128)(2,1)S(1)}, bf16[128,32]{0,1:T(8,128)(2,1)}, u32[]{:S(2)}) copy-start(bf16[128,32]{0,1:T(8,128)(2,1)} %param.16) | copy-start | bytes 24580
Sparse Core Ops, SparseCore 0:
  8.9 564.0 all-gather.3
  823.6 26.7 all-gather.5
  1282.1 36.0 all-reduce.2
  1331.6 38.4 all-reduce.4
  1382.5 561.1 all-gather.7
where the time goes:
time: 1990 us; the launch traced here: 1980 us
  waiting for transfers between devices  1170 us (59%)
  blocking collectives  383 us (19%)
  matrix products  224 us (11%)
  local copies, waits for them, and re-layouts  115 us (6%)
  other arithmetic  82.3 us (4%)
    all_gather x1, waiting for transfers between devices, local(): lax.all_gather(pair, 'gz', axis=0, tiled=True).astype(jnp.float32)  565 us
    all_gather x1, waiting for transfers between devices, local(): normed_mix = lax.all_gather(local_mix, 'gz', axis=0, tiled=True)  526 us
    all_to_all x1, blocking collectives, local(): lax.all_to_all(full_product, 'gx', split_axis=2, concat_axis=0, tiled=True)  191 us
    dot_general x4, matrix products, project(): jnp.einsum('cik,ch->hik', normed, weight, preferred_element_type=jnp.floa...  150 us
    all_to_all x1, blocking collectives, local(): lax.all_to_all(right_rows, 'gx', split_axis=0, concat_axis=2, tiled=True)  97.4 us
    all_to_all x1, blocking collectives, local(): lax.all_to_all(left_rows, 'gx', split_axis=0, concat_axis=2, tiled=True)  94.8 us
  transfers between devices with their start and end apart: 5, of which 4 were waited for; matrix products, arithmetic and copies ran while one was open for 7% of the time, Pallas kernels for 0%

commit v1 on v0

--- a/solution.py
+++ b/solution.py
@@ -56,7 +56,21 @@
     local_mix = (mix_centered * lax.rsqrt(mix_spread + epsilon) * out_gain[:, None, None]).astype(
         jnp.bfloat16
     )
-    normed_mix = lax.all_gather(local_mix, "gz", axis=0, tiled=True)
+
+    def cells_register(dimension_no, xs):
+        all_blocks = [xs]
+        num = lax.axis_size("gz")
+        for k0 in range(num - 1):
+            all_blocks.append(
+                lax.ppermute(all_blocks[-1], "gz", perm=[(h, (h + 1) % num) for h in range(num)])
+            )
+        work_now = jnp.concatenate(all_blocks[::-1], dimension_no)
+        arr_now = jnp.roll(
+            work_now, (lax.axis_index("gz") + 1) * xs.shape[dimension_no], dimension_no
+        )
+        return arr_now
+
+    normed_mix = cells_register(0, local_mix)
     projected = jnp.einsum("hij,hd->dij", normed_mix, w_out, preferred_element_type=jnp.float32)
     return (out_gate * projected).astype(jnp.bfloat16)
 

time: 1990 us -> 2050 us (1.030)
  local copies, waits for them, and re-layouts: 115 us -> 164 us
    all_gather x1 -> x0, waiting for transfers between devices: 526 us -> none  [local(): normed_mix = lax.all_gather(local_mix, 'gz', axis=0, tiled=True)]
    ppermute x0 -> x3, waiting for transfers between devices: none -> 509 us  [cells_register(): lax.ppermute(all_blocks[-1], 'gz', perm=[(h, (h + 1) % num) for h in rang...]
    unnamed x18 -> x26, local copies, waits for them, and re-layouts: 0.05 us -> 48.8 us
  transfers between devices with their start and end apart: 5 -> 7, of which waited for: 4 -> 6; matrix products, arithmetic and copies ran while one was open for 7% -> 6% of each run, Pallas kernels for 0% -> 0%
where the time goes in v1:
time: 2050 us; the launch traced here: 2040 us
  waiting for transfers between devices  1150 us (56%)
  blocking collectives  383 us (19%)
  matrix products  225 us (11%)
  local copies, waits for them, and re-layouts  164 us (8%)
  other arithmetic  102 us (5%)
    all_gather x1, waiting for transfers between devices, local(): lax.all_gather(pair, 'gz', axis=0, tiled=True).astype(jnp.float32)  565 us
    ppermute x3, waiting for transfers between devices, cells_register(): lax.ppermute(all_blocks[-1], 'gz', perm=[(h, (h + 1) % num) for h in rang...  509 us
    all_to_all x1, blocking collectives, local(): lax.all_to_all(full_product, 'gx', split_axis=2, concat_axis=0, tiled=True)  191 us
    dot_general x4, matrix products, project(): jnp.einsum('cik,ch->hik', normed, weight, preferred_element_type=jnp.floa...  149 us
    all_to_all x1, blocking collectives, local(): lax.all_to_all(right_rows, 'gx', split_axis=0, concat_axis=2, tiled=True)  97.4 us
    all_to_all x1, blocking collectives, local(): lax.all_to_all(left_rows, 'gx', split_axis=0, concat_axis=2, tiled=True)  94.8 us
    unnamed x26, local copies, waits for them, and re-layouts  48.8 us
  transfers between devices with their start and end apart: 7, of which 6 were waited for; matrix products, arithmetic and copies ran while one was open for 6% of the time, Pallas kernels for 0%

profile of v1, /device:TPU:0, one launch (start us, length us, event | category | flops | bytes accessed | tf_op | source)
XLA Modules:
  0.0 2038.4 jit_solution(6437507996356797742)
XLA Ops:
  8.4 564.6 %all-gather.3.cloned.1.call-done = bf16[128,512,256]{2,1,0:T(8,128)(2,1)} async-done(((bf16[32,512,256]{2,1,0:T(8,128)(2,1)}), bf16[128,512,256]{2,1,0:T(8,128)(2,1)}) %all-gather.3.cloned.1.call-update) | async-done | bytes 33554448 | tf_op jit(solution)/shard_map/all_gather | solution.py:21
  573.0 11.4 convert_reduce_fusion
  584.5 11.7 fusion.2
  596.2 23.0 %fusion.4 = bf16[128,512,256]{2,1,0:T(8,128)(2,1)} fusion(bf16[128,512,256]{2,1,0:T(8,128)(2,1)} %all-gather.3.cloned.1.call-done, f32[128]{0:T(128)S(1)} %copy-done.6, f32[512,256]{1,0:T(8,128)S(1)} %add_rsqrt_fusion.1, f32[512,256]{1,0:T(8,128)S(1)} %broadcast_multiply_fusion.1), kind=kLoop, calls=%fused_computation.6 | loop fusion | flops 83886080 | bytes 68157952 | tf_op jit(solution)/shard_map/convert_element_type | solution.py:25
  619.2 35.7 %fusion.13 = f32[512,256,32]{1,2,0:T(8,128)} fusion(bf16[128,512,256]{2,1,0:T(8,128)(2,1)} %fusion.4, bf16[128,32]{0,1:T(8,128)(2,1)S(1)} %copy-done), kind=kOutput, calls=%fused_computation.15 | convolution fusion | flops 1073741824 | bytes 50339840 | tf_op jit(solution)/shard_map/cik,ch->hik/dot_general | solution.py:29
  654.9 38.1 %fusion.34 = bf16[32,512,256]{2,0,1:T(8,128)(2,1)} fusion(bf16[128,512,256]{2,1,0:T(8,128)(2,1)} %fusion.4, f32[512,256,32]{1,2,0:T(8,128)} %fusion.13, f32[512,256]{1,0:T(8,128)S(1)} %convert_element_type.23, bf16[128,32]{0,1:T(8,128)(2,1)S(1)} %copy-done.7), kind=kOutput, calls=%fused_computation.34 | convolution fusion | flops 1098907648 | bytes 59252736 | tf_op jit(solution)/shard_map/cik,ch->hik/dot_general | solution.py:29
  693.0 11.4 copy.27
  704.4 97.4 %all_to_all.54 = bf16[32,512,256]{2,1,0:T(8,128)(2,1)S(1)} all-to-all(bf16[32,512,256]{2,1,0:T(8,128)(2,1)} %copy.27), channel_id=1, replica_groups=mesh['gx'=4,'gy'=2,'gz'=4] {'gx'}, dimensions={0} | all-to-all | bytes 16777216 | tf_op jit(solution)/shard_map/all_to_all | solution.py:42
  809.0 14.3 all_to_all.46
  823.4 37.6 %fusion.9 = f32[512,256,32]{1,2,0:T(8,128)} fusion(bf16[128,512,256]{2,1,0:T(8,128)(2,1)} %fusion.4, bf16[128,32]{0,1:T(8,128)(2,1)S(1)} %copy-done.3), kind=kOutput, calls=%fused_computation.11 | convolution fusion | flops 1073741824 | bytes 50339840 | tf_op jit(solution)/shard_map/cik,ch->hik/dot_general | solution.py:29
  861.0 38.1 %fusion.31 = bf16[32,512,256]{2,0,1:T(8,128)(2,1)} fusion(bf16[128,512,256]{2,1,0:T(8,128)(2,1)} %fusion.4, f32[512,256,32]{1,2,0:T(8,128)} %fusion.9, f32[512,256]{1,0:T(8,128)S(1)} %convert_element_type.23, bf16[128,32]{0,1:T(8,128)(2,1)S(1)} %copy-done.8), kind=kOutput, calls=%fused_computation.33 | convolution fusion | flops 1098907648 | bytes 59252736 | tf_op jit(solution)/shard_map/cik,ch->hik/dot_general | solution.py:29
  899.2 11.4 copy.23
  910.5 94.8 %all_to_all.55 = bf16[32,512,256]{2,1,0:T(8,128)(2,1)S(1)} all-to-all(bf16[32,512,256]{2,1,0:T(8,128)(2,1)} %copy.23), channel_id=1, replica_groups=mesh['gx'=4,'gy'=2,'gz'=4] {'gx'}, dimensions={0} | all-to-all | bytes 16777216 | tf_op jit(solution)/shard_map/all_to_all | solution.py:41
  1012.6 14.3 all_to_all.42
  1027.0 17.0 fusion.44
  1043.9 17.6 copy.29
  1061.5 190.6 %all_to_all.56 = f32[8,512,1024]{1,0,2:T(8,128)} all-to-all(f32[8,512,1024]{1,0,2:T(8,128)} %copy.29), channel_id=1, replica_groups=mesh['gx'=4,'gy'=2,'gz'=4] {'gx'}, dimensions={2} | all-to-all | bytes 33554432 | tf_op jit(solution)/shard_map/all_to_all | solution.py:50
  1252.1 20.2 copy.30
  1272.3 9.5 bitcast_reduce_fusion
  1281.9 36.0 %all-reduce.3.cloned.1.call-done = f32[512,256]{1,0:T(8,128)} async-done(((f32[512,256]{1,0:T(8,128)}), f32[512,256]{1,0:T(8,128)}) %all-reduce.3.cloned.1.call-update) | async-done | bytes 524304 | tf_op jit(solution)/shard_map/psum | solution.py:52
  1318.9 12.2 fusion.21
  1331.2 38.6 %all-reduce.5.cloned.1.call-done = f32[512,256]{1,0:T(8,128)} async-done(((f32[512,256]{1,0:T(8,128)}), f32[512,256]{1,0:T(8,128)}) %all-reduce.5.cloned.1.call-update) | async-done | bytes 524304 | tf_op jit(solution)/shard_map/psum | solution.py:55
  1370.9 8.7 fusion.19
  1381.2 181.5 %collective-permute-done = bf16[32,512,256]{2,0,1:T(8,128)(2,1)S(1)} collective-permute-done((bf16[32,512,256]{2,0,1:T(8,128)(2,1)S(1)}, bf16[32,512,256]{2,0,1:T(8,128)(2,1)S(1)}, u32[]{:S(2)}, u32[]{:S(2)}) %collective-permute-start) | collective-permute-done | bytes 8388640 | tf_op jit(solution)/shard_map/ppermute | solution.py:65
  1566.1 182.3 %collective-permute-done.1 = bf16[32,512,256]{2,0,1:T(8,128)(2,1)} collective-permute-done((bf16[32,512,256]{2,0,1:T(8,128)(2,1)S(1)}, bf16[32,512,256]{2,0,1:T(8,128)(2,1)}, u32[]{:S(2)}, u32[]{:S(2)}) %collective-permute-start.1) | collective-permute-done | bytes 8388640 | tf_op jit(solution)/shard_map/ppermute | solution.py:65
  1748.5 36.2 %fusion.7 = f32[512,256,32]{1,2,0:T(8,128)} fusion(bf16[128,512,256]{2,1,0:T(8,128)(2,1)} %fusion.4, bf16[128,32]{0,1:T(8,128)(2,1)S(1)} %copy-done.4), kind=kOutput, calls=%fused_computation.9 | convolution fusion | flops 1073741824 | bytes 50339840 | tf_op jit(solution)/shard_map/cij,cd->dij/dot_general | solution.py:38
  1784.7 145.4 %collective-permute-done.2 = bf16[32,512,256]{2,0,1:T(8,128)(2,1)} collective-permute-done((bf16[32,512,256]{2,0,1:T(8,128)(2,1)}, bf16[32,512,256]{2,0,1:T(8,128)(2,1)}, u32[]{:S(2)}, u32[]{:S(2)}) %collective-permute-start.2) | collective-permute-done | bytes 8388640 | tf_op jit(solution)/shard_map/ppermute | solution.py:65
  1937.7 7.6 constant_dynamic-update-slice_fusion.6
  1952.9 11.2 constant_dynamic-update-slice_fusion.4
  1986.7 11.2 constant_dynamic-update-slice_fusion
  1997.9 21.9 %fusion.28 = bf16[32,512,256]{2,0,1:T(8,128)(2,1)} fusion(bf16[256,512,256]{2,0,1:T(8,128)(2,1)} %constant_dynamic-update-slice_fusion, s32[]{:T(128)S(6)} %select_n.14, f32[512,256,32]{1,2,0:T(8,128)} %fusion.7, bf16[128,32]{0,1:T(8,128)(2,1)S(1)} %copy-done.9), kind=kOutput, calls=%fused_computation.32 | convolution fusion | flops 1094713344 | bytes 58728452 | tf_op jit(solution)/shard_map/hij,hd->dij/dot_general | solution.py:74
  2019.8 11.5 copy.31
  (44 shorter events, 61.7 us)
Async XLA Ops:
  6.5 612.7 %copy-start = (bf16[128,32]{0,1:T(8,128)(2,1)S(1)}, bf16[128,32]{0,1:T(8,128)(2,1)}, u32[]{:S(2)}) copy-start(bf16[128,32]{0,1:T(8,128)(2,1)} %param.16) | copy-start | bytes 24580
  6.5 566.5 %all-gather.3.cloned.1.call-start = ((), (), s32[]{:S(2)}) async-start(), calls=%async_computation.3 | async-start | bytes 41943040 | tf_op jit(solution)/shard_map/all_gather | solution.py:21
  7.3 1019.7 %all-gather.5.cloned.1.call-start = ((), (), s32[]{:S(2)}) async-start(), calls=%async_computation.4 | async-start | bytes 25165824 | tf_op jit(solution)/shard_map/all_gather | solution.py:46
  584.5 11.8 copy-start.6
  619.2 35.7 %copy-start.7 = (bf16[128,32]{0,1:T(8,128)(2,1)S(1)}, bf16[128,32]{0,1:T(8,128)(2,1)}, u32[]{:S(2)}) copy-start(bf16[128,32]{0,1:T(8,128)(2,1)} %param.15) | copy-start | bytes 24580
  809.0 14.4 copy-start.3
  823.4 37.7 %copy-start.8 = (bf16[128,32]{0,1:T(8,128)(2,1)S(1)}, bf16[128,32]{0,1:T(8,128)(2,1)}, u32[]{:S(2)}) copy-start(bf16[128,32]{0,1:T(8,128)(2,1)} %param.13) | copy-start | bytes 24580
  823.4 494.5 %all-reduce.3.cloned.1.call-start = ((), (), s32[]{:S(2)}) async-start(), calls=%async_computation.5 | async-start | bytes 1048576 | tf_op jit(solution)/shard_map/psum | solution.py:52
  1272.3 98.6 %copy-start.5 = (f32[32]{0:T(128)S(1)}, f32[32]{0:T(128)}, u32[]{:S(2)}) copy-start(f32[32]{0:T(128)} %param.18) | copy-start | bytes 388
  1281.8 87.9 %all-reduce.5.cloned.1.call-start = ((), (), s32[]{:S(2)}) async-start(), calls=%async_computation.6 | async-start | bytes 1048576 | tf_op jit(solution)/shard_map/psum | solution.py:55
  1331.1 417.3 %copy-start.4 = (bf16[128,32]{0,1:T(8,128)(2,1)S(1)}, bf16[128,32]{0,1:T(8,128)(2,1)}, u32[]{:S(2)}) copy-start(bf16[128,32]{0,1:T(8,128)(2,1)} %param.17) | copy-start | bytes 24580
  1379.6 183.1 %collective-permute-start = (bf16[32,512,256]{2,0,1:T(8,128)(2,1)S(1)}, bf16[32,512,256]{2,0,1:T(8,128)(2,1)S(1)}, u32[]{:S(2)}, u32[]{:S(2)}) collective-permute-start(bf16[32,512,256]{2,0,1:T(8,128)(2,1)S(1)} %fusion.19), channel_id=1, source_target_pairs={{0,1},{1,2},{2,3},{3,0},{4,5},{5,6},{6,7},{7,4},{8,9},{9,10},{10,1... | collective-permute-start | bytes 25165832 | tf_op jit(solution)/shard_map/ppermute | solution.py:65
  1562.7 3.4 copy-start.2
  1566.1 182.3 %collective-permute-start.1 = (bf16[32,512,256]{2,0,1:T(8,128)(2,1)S(1)}, bf16[32,512,256]{2,0,1:T(8,128)(2,1)}, u32[]{:S(2)}, u32[]{:S(2)}) collective-permute-start(bf16[32,512,256]{2,0,1:T(8,128)(2,1)S(1)} %collective-permute-done), channel_id=1, source_target_pairs={{0,1},{1,2},{2,3},{3,0},{4,5},{5,6},{6,7},{7,4},{8,9},{9,10},{10,1... | collective-permute-start | bytes 25165832 | tf_op jit(solution)/shard_map/ppermute | solution.py:65
  1748.5 181.7 %collective-permute-start.2 = (bf16[32,512,256]{2,0,1:T(8,128)(2,1)}, bf16[32,512,256]{2,0,1:T(8,128)(2,1)}, u32[]{:S(2)}, u32[]{:S(2)}) collective-permute-start(bf16[32,512,256]{2,0,1:T(8,128)(2,1)} %collective-permute-done.1), channel_id=1, source_target_pairs={{0,1},{1,2},{2,3},{3,0},{4,5},{5,6},{6,7},{7,4},{8,9},{9,10},{10,1... | collective-permute-start | bytes 25165832 | tf_op jit(solution)/shard_map/ppermute | solution.py:65
  1986.7 11.2 copy-start.9
  1997.9 33.5 %copy-start.1 = (bf16[128,32]{0,1:T(8,128)(2,1)S(1)}, bf16[128,32]{0,1:T(8,128)(2,1)}, u32[]{:S(2)}) copy-start(bf16[128,32]{0,1:T(8,128)(2,1)} %param.16) | copy-start | bytes 24580
Sparse Core Ops, SparseCore 0:
  8.9 564.0 all-gather.2
  823.5 26.7 all-gather.4
  1282.0 35.8 all-reduce.2
  1331.3 38.4 all-reduce.4
